TPU v7x, 32 devices: a whole 2x2x4 slice. The times are simulated.
32 devices in a mesh: dp: 2 (over y), expert: 4 (over z), ffn: 4 (over x, core).
Axes of the slice: x: 2, y: 2, z: 4, core: 2. Of those that a mesh axis runs over, the one named last changes fastest.
Arguments:
- tokens: bfloat16 [64, 6144], P(('dp', 'expert'), 'ffn'), may hold values from -6 to 6
- out_grad: bfloat16 [64, 6144], P(('dp', 'expert'), 'ffn'), may hold values from -6 to 6
- expert_ids: int32 [64, 2], P(('dp', 'expert')), may hold values from 0 to 3, all different within a row; in each aligned block of 8 rows (0 to 7, 8 to 15, ...) at most 6 rows name the same one
- tenant_ids: int32 [64], P(('dp', 'expert')), may hold values from 0 to 7
- router_logits: float32 [64, 2], P(('dp', 'expert')), may hold values from -8 to 8
- gate_projection_weight: bfloat16 [4, 6144, 8192], P('expert', None, ('dp', 'ffn')), may hold values from -0.078125 to 0.078125
- up_projection_weight: bfloat16 [4, 6144, 8192], P('expert', None, ('dp', 'ffn')), may hold values from -0.078125 to 0.078125
- down_projection_weight: bfloat16 [4, 8192, 6144], P('expert', ('dp', 'ffn')), may hold values from -0.0625 to 0.0625
- input_down_maps: bfloat16 [4, 6144, 256], P('expert', 'ffn'), may hold values from -0.078125 to 0.078125
- input_up_maps: bfloat16 [4, 2, 128, 8192], P('expert', None, None, ('dp', 'ffn')), may hold values from -1.5 to 1.5
- output_down_map: bfloat16 [4, 8192, 128], P('expert', ('dp', 'ffn')), may hold values from -0.0625 to 0.0625
- output_up_map: bfloat16 [4, 128, 6144], P('expert', None, 'ffn'), may hold values from -1.5 to 1.5
Outputs:
- mixed: bfloat16 [64, 6144], P(('dp', 'expert'), 'ffn')
- input_grad: bfloat16 [64, 6144], P(('dp', 'expert'), 'ffn')
- input_down_gradient: float32 [4, 6144, 256], P('expert', 'ffn')
- input_up_gradient: float32 [4, 2, 128, 8192], P('expert', None, None, ('dp', 'ffn'))
- output_down_gradient: float32 [4, 8192, 128], P('expert', ('dp', 'ffn'))
- output_up_gradient: float32 [4, 128, 6144], P('expert', None, 'ffn')
Inputs may be any that keep to these rules, and one draw needn't show every extreme that they name: `expert_ids`: each row names 2 different experts. Among the rows of one device's block of 8 tokens no expert is named more than 6 times; in some blocks one expert is named exactly 6 times.
All inputs are finite; a program needn't handle non-finite values.
Results may differ from a plain program's by a relative error of at most 0.0073.
Values may be sent and summed in bfloat16 or wider, within the bound.
A program may use at most 256 MiB of HBM per device.

v0:
```python
import jax
import jax.numpy as jnp
from jax import lax
from jax.sharding import PartitionSpec as P

RANK = 16


ADAPTER_SCALE = 0.5


def matrix_product(left, right):
    return jnp.dot(left, right, preferred_element_type=jnp.float32)


def backward_product(left, right):
    return lax.dot_general(
        left, right, (((1,), (1,)), ((), ())), preferred_element_type=jnp.float32
    )


def outside_rows(left, right):
    return lax.dot_general(
        left, right, (((0,), (0,)), ((), ())), preferred_element_type=jnp.float32
    )


def exact_product(left, right):
    return lax.dot_general(
        left,
        right,
        (((0,), (0,)), ((), ())),
        precision=lax.Precision.HIGHEST,
        preferred_element_type=jnp.float32,
    )


def slot_tables(expert_ids, router_logits, n_experts, capacity):
    tok_rows, n_top = expert_ids.shape
    flat_ids = expert_ids.reshape(-1)
    labels = jnp.arange(n_experts, dtype=jnp.int32)
    onehot = (flat_ids[:, None] == labels[None, :]).astype(jnp.int32)
    before = jnp.cumsum(onehot, axis=0) - onehot
    position = jnp.sum(before * onehot, axis=1)
    slot_index = flat_ids * capacity + position
    slot_ids = jnp.arange(n_experts * capacity, dtype=jnp.int32)
    chosen = (slot_index[None, :] == slot_ids[:, None]).astype(jnp.float32)
    chosen_rows = chosen.reshape(n_experts * capacity, tok_rows, n_top)
    prob_first = jax.nn.sigmoid(router_logits[:, 0] - router_logits[:, 1])
    gate_probs = jnp.stack([prob_first, 1.0 - prob_first], axis=1)
    picked = jnp.sum(chosen_rows, axis=2)
    weighted = jnp.sum(chosen_rows * gate_probs[None, :, :], axis=2)
    return (picked, weighted)


def per_device(
    tokens,
    out_grad,
    expert_ids,
    tenant_ids,
    router_logits,
    gate_projection_weight,
    up_projection_weight,
    down_projection_weight,
    input_down_maps,
    input_up_maps,
    output_down_map,
    output_up_map,
):
    n_experts = lax.axis_size("expert")
    n_data = lax.axis_size("dp")
    n_split = lax.axis_size("ffn")
    tok_rows = tokens.shape[0]
    capacity = 3 * tok_rows // n_experts
    quarter = tokens.shape[1]
    full_width = quarter * n_split
    hidden_dev = gate_projection_weight.shape[2]
    paired_columns = output_down_map.shape[2]
    block_rows = n_experts * capacity
    picked, weighted = slot_tables(expert_ids, router_logits, n_experts, capacity)
    tenant_slot = (
        jnp.dot(picked, (tenant_ids + 1).astype(jnp.float32), precision=lax.Precision.HIGHEST) - 1.0
    )
    tenant_send = tenant_slot.astype(jnp.bfloat16).reshape(n_experts, capacity)
    tok_send = (
        matrix_product(picked.astype(jnp.bfloat16), tokens)
        .astype(jnp.bfloat16)
        .reshape(n_experts, capacity, quarter)
    )
    grad_send = lax.dot_general(
        weighted,
        out_grad.astype(jnp.float32),
        (((1,), (0,)), ((), ())),
        precision=lax.Precision.HIGHEST,
        preferred_element_type=jnp.float32,
    )
    grad_send = grad_send.astype(jnp.bfloat16).reshape(n_experts, capacity, quarter)
    recv_tokens, recv_grads, recv_tenant = (
        lax.all_to_all(tok_send, "expert", split_axis=0, concat_axis=0, tiled=True),
        lax.all_to_all(grad_send, "expert", split_axis=0, concat_axis=0, tiled=True),
        lax.all_to_all(tenant_send, "expert", split_axis=0, concat_axis=0, tiled=True),
    )
    expert_tokens, expert_grads, expert_tenant = (
        lax.all_gather(recv_tokens, "dp", axis=0, tiled=True),
        lax.all_gather(recv_grads, "dp", axis=0, tiled=True),
        lax.all_gather(recv_tenant, "dp", axis=0, tiled=True),
    )
    portion_tokens = expert_tokens.reshape(-1, quarter)
    portion_gradients = expert_grads.reshape(-1, quarter)
    whole_tokens, whole_grads = (
        lax.all_gather(expert_tokens, "ffn", axis=2, tiled=True),
        lax.all_gather(expert_grads, "ffn", axis=2, tiled=True),
    )
    complete_tokens = whole_tokens.reshape(-1, full_width)
    complete_gradients = whole_grads.reshape(-1, full_width)
    row_tenant = expert_tenant.reshape(-1).astype(jnp.float32)
    column_tenant = (jnp.arange(paired_columns, dtype=jnp.int32) // RANK).astype(jnp.float32)
    tenant_column_mask = (row_tenant[:, None] == column_tenant[None, :]).astype(jnp.float32)
    paired_mask = jnp.concatenate([tenant_column_mask, tenant_column_mask], axis=1)
    adapter_input, adapter_backward = lax.psum(
        (
            matrix_product(portion_tokens, input_down_maps[0]),
            backward_product(portion_gradients, output_up_map[0]),
        ),
        "ffn",
    )
    adapter_rows = (paired_mask * adapter_input).astype(jnp.bfloat16)
    gate_activation = matrix_product(
        complete_tokens, gate_projection_weight[0]
    ) + ADAPTER_SCALE * matrix_product(adapter_rows[:, :paired_columns], input_up_maps[0, 0])
    up_activation = matrix_product(
        complete_tokens, up_projection_weight[0]
    ) + ADAPTER_SCALE * matrix_product(adapter_rows[:, paired_columns:], input_up_maps[0, 1])
    activated = jax.nn.silu(gate_activation)
    hidden_state = (activated * up_activation).astype(jnp.bfloat16)
    hidden_blocks = hidden_state.reshape(n_data, block_rows, hidden_dev)
    down_cols = down_projection_weight[0].reshape(hidden_dev, n_split, quarter)
    gate_cols = gate_projection_weight[0].reshape(n_split, quarter, hidden_dev)
    up_cols = up_projection_weight[0].reshape(n_split, quarter, hidden_dev)

    def block_ids(count):
        numbers = jnp.arange(count // block_rows, dtype=jnp.int32)
        return (numbers // n_split, numbers % n_split)

    row_ids, col_ids = block_ids(block_rows * lax.axis_size(("dp", "ffn")))
    lhs_rows = jnp.take(hidden_blocks, row_ids, axis=0)
    rhs_cols = jnp.take(down_cols, col_ids, axis=1)
    terms = jnp.einsum("brh,hbd->brd", lhs_rows, rhs_cols, preferred_element_type=jnp.float32)
    expert_portion = lax.psum_scatter(
        terms.reshape(block_rows * lax.axis_size(("dp", "ffn")), quarter),
        ("dp", "ffn"),
        scatter_dimension=0,
        tiled=True,
    )
    down_adapter_term = lax.psum(matrix_product(hidden_state, output_down_map[0]), ("dp", "ffn"))
    down_row_values = (tenant_column_mask * down_adapter_term).astype(jnp.bfloat16)
    backward_rows = (tenant_column_mask * adapter_backward).astype(jnp.bfloat16)
    hidden_gradient = backward_product(
        complete_gradients, down_projection_weight[0]
    ) + ADAPTER_SCALE * backward_product(backward_rows, output_down_map[0])
    output_down_gradient = ADAPTER_SCALE * outside_rows(hidden_state, backward_rows)
    output_up_gradient = ADAPTER_SCALE * outside_rows(down_row_values, portion_gradients)
    sigmoid_gate = jax.nn.sigmoid(gate_activation)
    gate_gradient = (
        hidden_gradient
        * up_activation
        * sigmoid_gate
        * (1.0 + gate_activation * (1.0 - sigmoid_gate))
    ).astype(jnp.bfloat16)
    up_gradient = (hidden_gradient * activated).astype(jnp.bfloat16)
    input_up_gradient = ADAPTER_SCALE * jnp.stack(
        [
            outside_rows(adapter_rows[:, :paired_columns], gate_gradient),
            outside_rows(adapter_rows[:, paired_columns:], up_gradient),
        ]
    )
    up_portion = jnp.concatenate(
        [
            backward_product(gate_gradient, input_up_maps[0, 0]),
            backward_product(up_gradient, input_up_maps[0, 1]),
        ],
        axis=1,
    )
    up_adapter_term = lax.psum(up_portion, ("dp", "ffn"))
    up_row_values = (paired_mask * up_adapter_term).astype(jnp.bfloat16)
    input_down_gradient = ADAPTER_SCALE * outside_rows(portion_tokens, up_row_values)
    gate_blocks = gate_gradient.reshape(n_data, block_rows, hidden_dev)
    up_blocks = up_gradient.reshape(n_data, block_rows, hidden_dev)
    row_ids, col_ids = block_ids(block_rows * lax.axis_size(("dp", "ffn")))
    gate_terms = jnp.einsum(
        "brh,bdh->brd",
        jnp.take(gate_blocks, row_ids, axis=0),
        jnp.take(gate_cols, col_ids, axis=0),
        preferred_element_type=jnp.float32,
    )
    up_terms = jnp.einsum(
        "brh,bdh->brd",
        jnp.take(up_blocks, row_ids, axis=0),
        jnp.take(up_cols, col_ids, axis=0),
        preferred_element_type=jnp.float32,
    )
    input_portion = lax.psum_scatter(
        (gate_terms + up_terms).reshape(block_rows * lax.axis_size(("dp", "ffn")), quarter),
        ("dp", "ffn"),
        scatter_dimension=0,
        tiled=True,
    )
    data_start = lax.axis_index("dp") * block_rows
    tenant_down = lax.dynamic_slice_in_dim(down_row_values, data_start, block_rows, 0)
    tenant_up = lax.dynamic_slice_in_dim(up_row_values, data_start, block_rows, 0)
    expert_output = (
        expert_portion + ADAPTER_SCALE * matrix_product(tenant_down, output_up_map[0])
    ).astype(jnp.bfloat16)
    input_result = (
        input_portion + ADAPTER_SCALE * backward_product(tenant_up, input_down_maps[0])
    ).astype(jnp.bfloat16)
    back_out, back_input = (
        lax.all_to_all(
            expert_output.reshape(n_experts, capacity, quarter),
            "expert",
            split_axis=0,
            concat_axis=0,
            tiled=True,
        ),
        lax.all_to_all(
            input_result.reshape(n_experts, capacity, quarter),
            "expert",
            split_axis=0,
            concat_axis=0,
            tiled=True,
        ),
    )
    mixed = exact_product(weighted, back_out.reshape(-1, quarter).astype(jnp.float32)).astype(
        jnp.bfloat16
    )
    input_grad = exact_product(picked, back_input.reshape(-1, quarter).astype(jnp.float32)).astype(
        jnp.bfloat16
    )
    return (
        mixed,
        input_grad,
        input_down_gradient[None],
        input_up_gradient[None],
        output_down_gradient[None],
        output_up_gradient[None],
    )


def solution(mesh):
    return jax.shard_map(
        per_device,
        mesh=mesh,
        in_specs=(
            P(("dp", "expert"), "ffn"),
            P(("dp", "expert"), "ffn"),
            P(("dp", "expert"), None),
            P(("dp", "expert")),
            P(("dp", "expert"), None),
            P("expert", None, ("dp", "ffn")),
            P("expert", None, ("dp", "ffn")),
            P("expert", ("dp", "ffn"), None),
            P("expert", "ffn", None),
            P("expert", None, None, ("dp", "ffn")),
            P("expert", ("dp", "ffn"), None),
            P("expert", None, "ffn"),
        ),
        out_specs=(
            P(("dp", "expert"), "ffn"),
            P(("dp", "expert"), "ffn"),
            P("expert", "ffn", None),
            P("expert", None, None, ("dp", "ffn")),
            P("expert", ("dp", "ffn"), None),
            P("expert", None, "ffn"),
        ),
        check_vma=False,
    )
```

profile of v0, /device:TPU:0, one launch (start us, length us, event | category | flops | bytes accessed | tf_op | source)
XLA Modules:
  0.0 311.2 jit_solution(11747754838168204780)
XLA Ops:
  7.2 0.8 copy.32
  8.6 0.8 broadcast_subtract_fusion
  9.4 0.8 fusion.33
  10.2 0.7 all_to_all.27
  10.9 6.3 %all-to-all-start.1 = ((bf16[4,1,6]{2,1,0:T(2,128)(2,1)}), bf16[4,1,6]{2,1,0:T(2,128)(2,1)S(1)}, u32[]{:S(2)}, u32[]{:S(2)}) async-start(bf16[4,1,6]{2,1,0:T(2,128)(2,1)} %all_to_all.27), calls=%async_computation.1 | async-start | bytes 4096 | tf_op jit(solution)/shard_map/all_to_all | solution.py:101
  17.3 16.6 %copy.36 = bf16[1,1024,6144]{1,2,0:T(8,128)(2,1)} copy(bf16[1,1024,6144]{2,1,0:T(8,128)(2,1)} %param.23) | data formatting | bytes 25165824 | tf_op args[7]
  33.9 10.4 %fusion.88 = (bf16[1024,4,768]{0,2,1:T(8,128)(2,1)}, bf16[1024,4,768]{0,2,1:T(8,128)(2,1)}) fusion(bf16[1024,4,1536]{0,2,1:T(8,128)(2,1)} %bitcast.92), kind=kLoop, calls=%fused_computation.155 | loop fusion | bytes 25165824 | tf_op jit(solution)/shard_map/jit(_take)/gather | solution.py:147
  44.3 8.8 %gather_fusion.1 = bf16[8,1024,768]{1,2,0:T(8,128)(2,1)} fusion(bf16[1024,4,768]{0,2,1:T(8,128)(2,1)} %get-tuple-element.21, s32[1024]{0:T(1024)S(1)} %pad_clamp_fusion.1), kind=kCustom, calls=%fused_computation.8 | custom fusion | bytes 25165856 | tf_op jit(solution)/shard_map/jit(_take)/gather | solution.py:147
  53.1 8.7 %gather_fusion = bf16[8,1024,768]{1,2,0:T(8,128)(2,1)} fusion(bf16[1024,4,768]{0,2,1:T(8,128)(2,1)} %get-tuple-element.20, s32[1024]{0:T(1024)S(1)} %pad_clamp_fusion.1), kind=kCustom, calls=%fused_computation.7 | custom fusion | bytes 25165856 | tf_op jit(solution)/shard_map/jit(_take)/gather | solution.py:147
  62.1 0.7 reshape.187
  62.9 0.7 reshape.180
  63.6 10.4 %fusion.87 = (bf16[4,768,1024]{2,1,0:T(8,128)(2,1)}, bf16[4,768,1024]{2,1,0:T(8,128)(2,1)}) fusion(bf16[4,1536,1024]{2,1,0:T(8,128)(2,1)} %bitcast.91), kind=kLoop, calls=%fused_computation.154 | loop fusion | bytes 25165824 | tf_op jit(solution)/shard_map/jit(_take)/gather | solution.py:193
  74.0 8.8 %gather_fusion.5 = bf16[8,768,1024]{2,1,0:T(8,128)(2,1)} fusion(bf16[4,768,1024]{2,1,0:T(8,128)(2,1)} %get-tuple-element.19, s32[1024]{0:T(1024)S(1)} %pad_clamp_fusion), kind=kCustom, calls=%fused_computation.2.clone | custom fusion | bytes 25165856 | tf_op jit(solution)/shard_map/jit(_take)/gather | solution.py:193
  82.8 8.7 %gather_fusion.4 = bf16[8,768,1024]{2,1,0:T(8,128)(2,1)} fusion(bf16[4,768,1024]{2,1,0:T(8,128)(2,1)} %get-tuple-element.18, s32[1024]{0:T(1024)S(1)} %pad_clamp_fusion), kind=kCustom, calls=%fused_computation.1.clone | custom fusion | bytes 25165856 | tf_op jit(solution)/shard_map/jit(_take)/gather | solution.py:193
  91.5 10.4 %fusion.86 = (bf16[4,768,1024]{2,1,0:T(8,128)(2,1)}, bf16[4,768,1024]{2,1,0:T(8,128)(2,1)}) fusion(bf16[4,1536,1024]{2,1,0:T(8,128)(2,1)} %bitcast.90), kind=kLoop, calls=%fused_computation.153 | loop fusion | bytes 25165824 | tf_op jit(solution)/shard_map/jit(_take)/gather | solution.py:199
  102.0 8.7 %gather_fusion.8 = bf16[8,768,1024]{2,1,0:T(8,128)(2,1)} fusion(bf16[4,768,1024]{2,1,0:T(8,128)(2,1)} %get-tuple-element.17, s32[1024]{0:T(1024)S(1)} %pad_clamp_fusion), kind=kCustom, calls=%fused_computation.6.clone | custom fusion | bytes 25165856 | tf_op jit(solution)/shard_map/jit(_take)/gather | solution.py:199
  110.7 8.7 %gather_fusion.7 = bf16[8,768,1024]{2,1,0:T(8,128)(2,1)} fusion(bf16[4,768,1024]{2,1,0:T(8,128)(2,1)} %get-tuple-element.16, s32[1024]{0:T(1024)S(1)} %pad_clamp_fusion), kind=kCustom, calls=%fused_computation.5.clone | custom fusion | bytes 25165856 | tf_op jit(solution)/shard_map/jit(_take)/gather | solution.py:199
  119.3 5.1 %all-to-all-start.3 = ((bf16[4,6,1536]{2,1,0:T(8,128)(2,1)}), bf16[4,6,1536]{2,1,0:T(8,128)(2,1)S(1)}, u32[]{:S(2)}, u32[]{:S(2)}) async-start(bf16[4,6,1536]{2,1,0:T(8,128)(2,1)} %reshape.187), calls=%async_computation.4 | async-start | bytes 196608 | tf_op jit(solution)/shard_map/all_to_all | solution.py:100
  124.4 4.4 %all-gather = bf16[8,1,6]{2,1,0:T(2,128)(2,1)S(1)} all-gather(bf16[4,1,6]{2,1,0:T(2,128)(2,1)S(1)} %all-to-all-done.1), channel_id=2, replica_groups=mesh['dp'=2,'expert'=4,'ffn'=4] {'dp'}, dimensions={0}, use_global_device_ids=true | all-gather | bytes 144 | tf_op jit(solution)/shard_map/all_gather | solution.py:106
  129.0 1.3 all-to-all-done.3
  130.3 3.8 %all-to-all-start = ((bf16[4,6,1536]{2,1,0:T(8,128)(2,1)}), bf16[4,6,1536]{2,1,0:T(8,128)(2,1)S(1)}, u32[]{:S(2)}, u32[]{:S(2)}) async-start(bf16[4,6,1536]{2,1,0:T(8,128)(2,1)} %reshape.180), calls=%async_computation | async-start | bytes 196608 | tf_op jit(solution)/shard_map/all_to_all | solution.py:99
  134.1 5.3 %all_gather.18 = bf16[8,6,1536]{2,1,0:T(8,128)(2,1)S(1)} all-gather(bf16[4,6,1536]{2,1,0:T(8,128)(2,1)S(1)} %all-to-all-done.3), channel_id=1, replica_groups=mesh['dp'=2,'expert'=4,'ffn'=4] {'dp'}, dimensions={0}, use_global_device_ids=true | all-gather | bytes 221184 | tf_op jit(solution)/shard_map/all_gather | solution.py:105
  139.4 8.6 %all_gather.19 = bf16[8,6,6144]{2,1,0:T(8,128)(2,1)S(1)} all-gather(bf16[8,6,1536]{2,1,0:T(8,128)(2,1)S(1)} %all_gather.18), channel_id=1, replica_groups=mesh['dp'=2,'expert'=4,'ffn'=4] {'ffn'}, dimensions={2}, use_global_device_ids=true | all-gather | bytes 737280 | tf_op jit(solution)/shard_map/all_gather | solution.py:112
  148.0 5.7 %all_gather.15 = bf16[8,6,1536]{2,1,0:T(8,128)(2,1)S(1)} all-gather(bf16[4,6,1536]{2,1,0:T(8,128)(2,1)S(1)} %all-to-all-done), channel_id=1, replica_groups=mesh['dp'=2,'expert'=4,'ffn'=4] {'dp'}, dimensions={0}, use_global_device_ids=true | all-gather | bytes 221184 | tf_op jit(solution)/shard_map/all_gather | solution.py:104
  153.8 8.0 %all_gather.16 = bf16[8,6,6144]{2,1,0:T(8,128)(2,1)S(1)} all-gather(bf16[8,6,1536]{2,1,0:T(8,128)(2,1)S(1)} %all_gather.15), channel_id=1, replica_groups=mesh['dp'=2,'expert'=4,'ffn'=4] {'ffn'}, dimensions={2}, use_global_device_ids=true | all-gather | bytes 737280 | tf_op jit(solution)/shard_map/all_gather | solution.py:111
  162.0 6.9 %fusion.14 = f32[48,1024]{1,0:T(8,128)S(1)} fusion(bf16[48,6144]{1,0:T(8,128)(2,1)S(1)} %reshape.181, bf16[1,6144,1024]{2,1,0:T(8,128)(2,1)} %param.22), kind=kOutput, calls=%fused_computation.26 | convolution fusion | flops 603979776 | bytes 13369344 | tf_op jit(solution)/shard_map/dot_general | solution.py:13
  168.9 7.6 %fusion.16 = f32[48,1024]{1,0:T(8,128)} fusion(bf16[48,6144]{1,0:T(8,128)(2,1)S(1)} %reshape.181, bf16[1,6144,1024]{2,1,0:T(8,128)(2,1)} %param.21), kind=kOutput, calls=%fused_computation.28 | convolution fusion | flops 603979776 | bytes 13369344 | tf_op jit(solution)/shard_map/dot_general | solution.py:13
  176.7 8.5 %fusion.12 = f32[48,1024]{1,0:T(8,128)S(1)} fusion(bf16[48,6144]{1,0:T(8,128)(2,1)S(1)} %reshape.188, bf16[1,1024,6144]{2,1,0:T(8,128)(2,1)} %param.23), kind=kOutput, calls=%fused_computation.24 | convolution fusion | flops 603979776 | bytes 13369344 | tf_op jit(solution)/shard_map/dot_general | solution.py:17
  185.7 12.1 %all-reduce.1 = (bf16[48,256]{1,0:T(8,128)(2,1)S(1)}, bf16[48,128]{1,0:T(8,128)(2,1)S(1)}) all-reduce(f32[48,256]{1,0:T(8,128)S(1)} %fusion.35, f32[48,128]{1,0:T(8,128)S(1)} %fusion.37), channel_id=1, replica_groups=mesh['dp'=2,'expert'=4,'ffn'=4] {'ffn'}, use_global_device_ids=true, to_apply=%region_4.5 | all-reduce | flops 18432 | bytes 110592 | tf_op jit(solution)/shard_map/psum | solution.py:120
  198.3 1.2 multiply_convert_fusion.1
  199.5 1.3 gather_fusion.2
  200.8 12.7 %fusion = f32[8,24,1536]{2,1,0:T(8,128)} fusion(bf16[1024,8,768]{0,2,1:T(8,128)(2,1)} %bitcast.93, bf16[1024,8,768]{0,2,1:T(8,128)(2,1)} %bitcast.94, pred[8]{0:T(512)(128)(4,1)S(1)} %get-tuple-element.28, bf16[8,24,1024]{2,1,0:T(8,128)(2,1)} %gather_fusion.2, pred[8]{0:T(512)(128)(4,1)S(1)} %get-tuple-element.27), kind=kOutput, calls=%fused_computation.10 | convolution fusion | flops 667090944 | bytes 26738704 | tf_op jit(solution)/shard_map/brh,hbd->brd/dot_general | solution.py:148
  215.4 11.7 %fusion.3 = f32[8,24,1536]{2,1,0:T(8,128)S(1)} fusion(bf16[8,768,1024]{2,1,0:T(8,128)(2,1)} %gather_fusion.5, bf16[8,768,1024]{2,1,0:T(8,128)(2,1)} %gather_fusion.4, pred[8]{0:T(512)(128)(4,1)S(1)} %get-tuple-element.28, bf16[8,24,1024]{2,1,0:T(8,128)(2,1)S(1)} %gather_fusion.3, pred[8]{0:T(512)(128)(4,1)S(1)} %get-tuple-element.27), kind=kOutput, calls=%fused_computation.14 | convolution fusion | flops 667090944 | bytes 26738704 | tf_op jit(solution)/shard_map/brh,bdh->brd/dot_general | solution.py:190
  227.0 12.9 %fusion.22 = f32[8,24,1536]{2,1,0:T(8,128)} fusion(f32[8,24,1536]{2,1,0:T(8,128)S(1)} %fusion.3, bf16[8,768,1024]{2,1,0:T(8,128)(2,1)} %gather_fusion.8, bf16[8,768,1024]{2,1,0:T(8,128)(2,1)} %gather_fusion.7, pred[8]{0:T(512)(128)(4,1)S(1)} %get-tuple-element.28, bf16[8,24,1024]{2,1,0:T(8,128)(2,1)S(1)} %gather_fusion.6, pred[8]{0:T(512)(128)(4,1)S(1)} %get-tuple-element.27), kind=kOutput, calls=%fused_computation.35 | convolution fusion | flops 667385856 | bytes 27918352 | tf_op jit(solution)/shard_map/brh,bdh->brd/dot_general | solution.py:196
  240.1 23.9 %all-reduce = (bf16[48,128]{1,0:T(8,128)(2,1)S(1)}, bf16[48,256]{1,0:T(8,128)(2,1)S(1)}) all-reduce(f32[48,128]{1,0:T(8,128)S(1)} %fusion.47, f32[48,256]{1,0:T(8,128)S(1)} %pad_maximum_fusion), channel_id=1, replica_groups=mesh['dp'=2,'expert'=4,'ffn'=4] {'dp','ffn'}, use_global_device_ids=true, to_apply=%region_6.8 | all-reduce | flops 18432 | bytes 110592 | tf_op jit(solution)/shard_map/psum | solution.py:155
  264.6 1.1 fusion.28
  265.7 1.2 fusion.23
  266.9 1.6 fusion.21
  268.4 1.1 maximum_multiply_fusion
  269.5 1.1 fusion.26
  271.3 5.2 %all-to-all-start.2 = ((bf16[4,6,1536]{2,1,0:T(8,128)(2,1)}), bf16[4,6,1536]{2,1,0:T(8,128)(2,1)S(1)}, u32[]{:S(2)}, u32[]{:S(2)}) async-start(bf16[4,6,1536]{2,1,0:T(8,128)(2,1)} %reshape.185), calls=%async_computation.3 | async-start | bytes 196608 | tf_op jit(solution)/shard_map/all_to_all | solution.py:218
  276.5 14.7 %reduce-scatter.5.cloned.1.call-done = f32[24,1536]{1,0:T(8,128)} async-done(((f32[192,1536]{1,0:T(8,128)}), f32[24,1536]{1,0:T(8,128)}) %reduce-scatter.5.cloned.1.call-update) | async-done | bytes 147472 | tf_op jit(solution)/shard_map/reduce_scatter | solution.py:202
  291.2 1.2 fusion.27
  292.4 0.7 reshape.193
  293.1 4.6 %all-to-all-start.4 = ((bf16[4,6,1536]{2,1,0:T(8,128)(2,1)}), bf16[4,6,1536]{2,1,0:T(8,128)(2,1)S(1)}, u32[]{:S(2)}, u32[]{:S(2)}) async-start(bf16[4,6,1536]{2,1,0:T(8,128)(2,1)} %reshape.193), calls=%async_computation.6 | async-start | bytes 196608 | tf_op jit(solution)/shard_map/all_to_all | solution.py:225
  297.7 0.8 convolution_convert_fusion.3
  298.5 5.0 %all-to-all-done.4 = bf16[4,6,1536]{2,1,0:T(8,128)(2,1)S(1)} async-done(((bf16[4,6,1536]{2,1,0:T(8,128)(2,1)}), bf16[4,6,1536]{2,1,0:T(8,128)(2,1)S(1)}, u32[]{:S(2)}, u32[]{:S(2)}) %all-to-all-start.4) | async-done | bytes 73760 | tf_op jit(solution)/shard_map/all_to_all | solution.py:225
  303.6 0.8 convolution_convert_fusion.2
  (63 shorter events, 6.0 us)
Async XLA Ops:
  7.2 178.0 %copy-start = (bf16[1,1536,256]{2,1,0:T(8,128)(2,1)S(1)}, bf16[1,1536,256]{2,1,0:T(8,128)(2,1)}, u32[]{:S(2)}) copy-start(bf16[1,1536,256]{2,1,0:T(8,128)(2,1)} %param.24) | copy-start | bytes 2359300
  10.9 108.5 %all-to-all-start.1 = ((bf16[4,1,6]{2,1,0:T(2,128)(2,1)}), bf16[4,1,6]{2,1,0:T(2,128)(2,1)S(1)}, u32[]{:S(2)}, u32[]{:S(2)}) async-start(bf16[4,1,6]{2,1,0:T(2,128)(2,1)} %all_to_all.27), calls=%async_computation.1 | async-start | bytes 4096 | tf_op jit(solution)/shard_map/all_to_all | solution.py:101
  53.1 8.7 %copy-start.4 = (bf16[8,1536]{1,0:T(8,128)(2,1)S(1)}, bf16[8,1536]{1,0:T(8,128)(2,1)}, u32[]{:S(2)}) copy-start(bf16[8,1536]{1,0:T(8,128)(2,1)} %param.17) | copy-start | bytes 73732
  53.1 9.7 %copy-start.5 = (bf16[8,1536]{1,0:T(8,128)(2,1)S(1)}, bf16[8,1536]{1,0:T(8,128)(2,1)}, u32[]{:S(2)}) copy-start(bf16[8,1536]{1,0:T(8,128)(2,1)} %param.16) | copy-start | bytes 73732
  119.3 10.9 %all-to-all-start.3 = ((bf16[4,6,1536]{2,1,0:T(8,128)(2,1)}), bf16[4,6,1536]{2,1,0:T(8,128)(2,1)S(1)}, u32[]{:S(2)}, u32[]{:S(2)}) async-start(bf16[4,6,1536]{2,1,0:T(8,128)(2,1)} %reshape.187), calls=%async_computation.4 | async-start | bytes 196608 | tf_op jit(solution)/shard_map/all_to_all | solution.py:100
  130.3 17.7 %all-to-all-start = ((bf16[4,6,1536]{2,1,0:T(8,128)(2,1)}), bf16[4,6,1536]{2,1,0:T(8,128)(2,1)S(1)}, u32[]{:S(2)}, u32[]{:S(2)}) async-start(bf16[4,6,1536]{2,1,0:T(8,128)(2,1)} %reshape.180), calls=%async_computation | async-start | bytes 196608 | tf_op jit(solution)/shard_map/all_to_all | solution.py:99
  134.1 135.5 %reduce-scatter.3.cloned.1.call-start = ((), (), s32[]{:S(2)}) async-start(), calls=%async_computation.7 | async-start | bytes 1327104 | tf_op jit(solution)/shard_map/reduce_scatter | solution.py:149
  176.5 9.0 %copy-start.1 = (bf16[1,128,1536]{2,1,0:T(8,128)(2,1)S(1)}, bf16[1,128,1536]{2,1,0:T(8,128)(2,1)}, u32[]{:S(2)}) copy-start(bf16[1,128,1536]{2,1,0:T(8,128)(2,1)} %param.27) | copy-start | bytes 1179652
  176.5 21.4 %copy-start.3 = (bf16[1,1024,128]{2,1,0:T(8,128)(2,1)S(1)}, bf16[1,1024,128]{2,1,0:T(8,128)(2,1)}, u32[]{:S(2)}) copy-start(bf16[1,1024,128]{2,1,0:T(8,128)(2,1)} %param.26) | copy-start | bytes 786436
  176.7 21.4 %copy-start.2 = (bf16[1,2,128,1024]{3,2,1,0:T(8,128)(2,1)S(1)}, bf16[1,2,128,1024]{3,2,1,0:T(8,128)(2,1)}, u32[]{:S(2)}) copy-start(bf16[1,2,128,1024]{3,2,1,0:T(8,128)(2,1)} %param.25) | copy-start | bytes 1572868
  213.5 77.6 %reduce-scatter.5.cloned.1.call-start = ((), (), s32[]{:S(2)}) async-start(), calls=%async_computation.8 | async-start | bytes 1327104 | tf_op jit(solution)/shard_map/reduce_scatter | solution.py:202
  271.3 21.8 %all-to-all-start.2 = ((bf16[4,6,1536]{2,1,0:T(8,128)(2,1)}), bf16[4,6,1536]{2,1,0:T(8,128)(2,1)S(1)}, u32[]{:S(2)}, u32[]{:S(2)}) async-start(bf16[4,6,1536]{2,1,0:T(8,128)(2,1)} %reshape.185), calls=%async_computation.3 | async-start | bytes 196608 | tf_op jit(solution)/shard_map/all_to_all | solution.py:218
  293.1 10.4 %all-to-all-start.4 = ((bf16[4,6,1536]{2,1,0:T(8,128)(2,1)}), bf16[4,6,1536]{2,1,0:T(8,128)(2,1)S(1)}, u32[]{:S(2)}, u32[]{:S(2)}) async-start(bf16[4,6,1536]{2,1,0:T(8,128)(2,1)} %reshape.193), calls=%async_computation.6 | async-start | bytes 196608 | tf_op jit(solution)/shard_map/all_to_all | solution.py:225
Sparse Core Ops, SparseCore 0:
  213.6 37.5 reduce-scatter.2
  254.4 36.6 reduce-scatter.4
where the time goes:
time: 313 us; the launch traced here: 311 us
  local copies, waits for them, and re-layouts  108 us (35%)
  matrix products  72.1 us (23%)
  blocking collectives  68 us (22%)
  starting transfers between devices  25.4 us (8%)
  waiting for transfers between devices  21 us (7%)
  between operations  14.3 us (5%)
    gather x3, local copies, waits for them, and re-layouts, per_device(): jnp.take(gate_cols, col_ids, axis=0)  27.9 us
    gather x3, local copies, waits for them, and re-layouts, per_device(): rhs_cols = jnp.take(down_cols, col_ids, axis=1)  27.9 us
    gather x3, local copies, waits for them, and re-layouts, per_device(): jnp.take(up_cols, col_ids, axis=0)  27.8 us
    psum x1, blocking collectives, per_device(): lax.psum(matrix_product(hidden_state, output_down_map[0]), ('dp', 'ffn'))  23.9 us
    unnamed x14, local copies, waits for them, and re-layouts  17.5 us
    dot_general x8, matrix products, matrix_product(): return jnp.dot(left, right, preferred_element_type=jnp.float32)  17.5 us
    reduce_scatter x1, waiting for transfers between devices, per_device(): lax.psum_scatter((gate_terms + up_terms).reshape(block_rows * lax.axis_si...  14.7 us
    dot_general x1, matrix products, per_device(): jnp.einsum('brh,bdh->brd', jnp.take(up_blocks, row_ids, axis=0), jnp.take...  12.9 us
  transfers between devices with their start and end apart: 7, of which 3 were waited for; matrix products, arithmetic and copies ran while one was open for 44% of the time, Pallas kernels for 0%

commit v1 on v0

v1 whole, which is shorter than its diff:
```python
import functools

import jax
import jax.numpy as jnp
from jax import lax
from jax.experimental import pallas as pl
from jax.experimental.pallas import tpu as pltpu
from jax.sharding import PartitionSpec as P

RANK = 16
SCALE = 0.5
F32 = jnp.float32
BF16 = jnp.bfloat16
HIGH = lax.Precision.HIGHEST


def dot(a, b, dims=((1,), (0,)), precision=None):
    return lax.dot_general(
        a, b, (dims, ((), ())), preferred_element_type=F32, precision=precision
    )


def dot_nt(a, b, precision=None):
    return dot(a, b, ((1,), (1,)), precision)


def dot_tn(a, b):
    return dot(a, b, ((0,), (0,)))


def flip(index, mask):
    bit = 1
    while bit <= mask:
        if mask & bit:
            index = index + bit - 2 * bit * ((index // bit) % 2)
        bit *= 2
    return index


def bits_of(size):
    assert size & (size - 1) == 0
    return [1 << i for i in range(size.bit_length() - 1)]


def combos(bits):
    out = [0]
    for b in bits:
        out = out + [m | b for m in out]
    return out


def layer_kernel(
    nd, ne, nf,
    src, msk, wts, wg_hbm, wu_hbm, wd_hbm, idm, iup, odm, oum,
    mixed, igrad, idg, iug, odg, oug,
    gath, masks, xb, yb, wg, wu, wd, gate, up, hid, dgr, dur,
    q_s, vq_s, qz_s, wq_s, back, home,
    ar1s, ar1r, ar2s, ar2r, *rest,
):
    fbits, dbits = bits_of(nf), bits_of(nd)
    n_rs = len(fbits) + len(dbits)
    yr, xr = rest[:n_rs], rest[n_rs : 2 * n_rs]
    wsem, lsem, ssem, rsem = rest[2 * n_rs :]
    d, e, f = lax.axis_index("dp"), lax.axis_index("expert"), lax.axis_index("ffn")
    quarter = src.shape[2]
    hidden = wg.shape[2]
    rows_d = ne * 8
    rows = nd * rows_d
    cw = min(256, hidden)
    n_hc = hidden // cw
    qw = 256 if quarter % 256 == 0 else 128
    n_qc = quarter // qw
    pending = []
    counter = [0]

    def send(s, t, dev):
        i = counter[0]
        counter[0] += 1
        c = pltpu.make_async_remote_copy(
            src_ref=s, dst_ref=t, send_sem=ssem.at[i], recv_sem=rsem.at[i],
            device_id=dev, device_id_type=pl.DeviceIdType.MESH,
        )
        c.start()
        pending.append(c)
        return c

    arrival = [0]
    for b in reversed(fbits):
        arrival = arrival + [m | b for m in arrival]
    wcopies = []
    k = 0
    for m in arrival:
        qq = flip(f, m)
        pair = []
        for hbm, v in ((wg_hbm, wg), (wu_hbm, wu)):
            c = pltpu.make_async_copy(
                hbm.at[0, pl.ds(pl.multiple_of(qq * quarter, 128), quarter), :],
                v.at[qq], wsem.at[k],
            )
            c.start()
            k += 1
            pair.append(c)
        wcopies.append(pair)
    wd_copy = pltpu.make_async_copy(wd_hbm.at[0], wd, wsem.at[k])
    wd_copy.start()

    own = [
        pltpu.make_async_copy(src.at[e], gath.at[f, d, e], lsem.at[0]),
        pltpu.make_async_copy(msk.at[e], masks.at[d, e], lsem.at[1]),
    ]
    for c in own:
        c.start()

    barrier = pltpu.get_barrier_semaphore()
    peers = [(d, (e + j) % ne, f) for j in range(1, ne)]
    peers += [(flip(d, b), e, f) for b in dbits]
    peers += [(d, e, flip(f, b)) for b in fbits]
    for p in peers:
        pl.semaphore_signal(barrier, inc=1, device_id=p, device_id_type=pl.DeviceIdType.MESH)
    pl.semaphore_wait(barrier, len(peers))

    got = []
    for j in range(1, ne):
        to = (e + j) % ne
        got.append(send(src.at[to], gath.at[f, d, e], (d, to, f)))
        got.append(send(msk.at[to], masks.at[d, e], (d, to, f)))
    for c in own:
        c.wait()
    for c in got:
        c.wait_recv()

    top = fbits[-1] if fbits else 0
    early = []
    if top:
        early.append(send(gath.at[f, d], gath.at[f, d], (d, e, flip(f, top))))
    held = [0]
    for b in dbits:
        got = []
        for m in held:
            dm = flip(d, m)
            got.append(send(gath.at[f, dm], gath.at[f, dm], (flip(d, b), e, f)))
            got.append(send(masks.at[dm], masks.at[dm], (flip(d, b), e, f)))
        for c in got:
            c.wait_recv()
        if top:
            for m in held:
                dm = flip(d, b | m)
                early.append(send(gath.at[f, dm], gath.at[f, dm], (d, e, flip(f, top))))
        held = held + [m | b for m in held]

    half = ne // 2
    ys, xs = gath.at[:, :, :half], gath.at[:, :, half:]

    def unpack(q):
        def body(p, carry):
            dd, ee = p // half, (p % half) * 2
            v0 = gath[q, dd, ee].astype(F32)
            v1 = gath[q, dd, ee + 1].astype(F32)
            at = pl.ds(pl.multiple_of(p * 16, 16), 16)
            xb[q, at, :] = jnp.concatenate([v0[:8], v1[:8]], axis=0).astype(BF16)
            yb[q, at, :] = jnp.concatenate([v0[8:], v1[8:]], axis=0).astype(BF16)
            return carry

        lax.fori_loop(0, nd * half, body, 0)

    mask = masks[...].reshape(rows, masks.shape[3])
    ntr = mask.shape[1]
    mask3 = jnp.concatenate([mask, mask, mask], axis=1)
    lanes = 128
    col = lax.broadcasted_iota(jnp.int32, (3 * ntr, lanes), 0)
    lane = lax.broadcasted_iota(jnp.int32, (3 * ntr, lanes), 1)
    select = ((col // ntr) * RANK + col % RANK == lane).astype(F32)

    def compress(v):
        return dot(v * mask3, select, precision=HIGH)

    def expand(v):
        return dot_nt(v, select, precision=HIGH) * mask3

    def all_reduce(v, axes, sbuf, rbuf):
        for i, (axis, b) in enumerate(axes):
            sbuf[i] = v
            dev = (d, e, flip(f, b)) if axis == "f" else (flip(d, b), e, f)
            c = send(sbuf.at[i], rbuf.at[i], dev)
            yield
            c.wait_recv()
            v = v + rbuf[i]
        yield v

    def finish(gen):
        v = None
        for v in gen:
            pass
        return v

    unpack(f)
    pv = jnp.concatenate([dot(xb[f], idm[0]), dot_nt(yb[f], oum[0])], axis=1)
    ar1 = all_reduce(compress(pv), [("f", b) for b in reversed(fbits)], ar1s, ar1r)
    next(ar1)

    def project(m, first):
        q = flip(f, m)
        wcopies[arrival.index(m)][0].wait()
        wcopies[arrival.index(m)][1].wait()

        def body(c, carry):
            at = pl.ds(pl.multiple_of(c * cw, cw), cw)
            x = xb[q]
            g = dot(x, wg[q, :, at])
            u = dot(x, wu[q, :, at])
            if first:
                gate[:, at] = g
                up[:, at] = u
            else:
                gate[:, at] += g
                up[:, at] += u
            return carry

        lax.fori_loop(0, n_hc, body, 0)

    project(0, True)
    ready = [0]
    for n, b in enumerate(reversed(fbits)):
        if n == 0:
            got = early
        else:
            got = []
            for m in ready:
                qm = flip(f, m)
                got.append(send(gath.at[qm], gath.at[qm], (d, e, flip(f, b))))
        for c in got:
            c.wait_recv()
        ready = ready + [m | b for m in ready]
        if n + 1 < len(fbits):
            continue
    v = finish(ar1)
    pv = expand(v)
    q_s[...] = pv[:, : 2 * ntr].astype(BF16)
    vq_s[...] = pv[:, 2 * ntr :].astype(BF16)
    for m in arrival[1:]:
        unpack(flip(f, m))
        project(m, False)

    def activate(c, carry):
        at = pl.ds(pl.multiple_of(c * cw, cw), cw)
        g = gate[:, at] + SCALE * dot(q_s[:, :ntr], iup[0, 0, :, at])
        u = up[:, at] + SCALE * dot(q_s[:, ntr:], iup[0, 1, :, at])
        gate[:, at] = g
        up[:, at] = u
        hid[:, at] = (g * jax.nn.sigmoid(g) * u).astype(BF16)
        return carry

    lax.fori_loop(0, n_hc, activate, 0)

    def reduce_scatter(slabs, rbufs, produce):
        rec = {}
        for i, b in enumerate(fbits):
            ms = combos(fbits[i + 1 :])
            for n, m in enumerate(ms):
                add(slabs, rec, rbufs, i, b | m, produce)
                q = flip(f, b | m)
                rec[(i, m)] = (send(slabs.at[q], rbufs[i].at[n], (d, e, flip(f, b))), n)
                yield
        add(slabs, rec, rbufs, len(fbits), 0, produce)
        yield
        drec = {}
        for i, b in enumerate(dbits):
            r = rbufs[len(fbits) + i]
            ms = combos(dbits[i + 1 :])
            for n, m in enumerate(ms):
                dm = flip(d, b | m)
                for j in range(i):
                    c, pos = drec[(j, b | m)]
                    c.wait_recv()
                    slabs[f, dm] = (
                        slabs[f, dm].astype(F32) + rbufs[len(fbits) + j][pos].astype(F32)
                    ).astype(BF16)
                drec[(i, m)] = (send(slabs.at[f, dm], r.at[n], (flip(d, b), e, f)), n)
        yield
        total = slabs[f, d].astype(F32)
        for i in range(len(dbits)):
            c, pos = drec[(i, 0)]
            c.wait_recv()
            total = total + rbufs[len(fbits) + i][pos].astype(F32)
        yield total.reshape(rows_d, quarter)

    def add(slabs, rec, rbufs, upto, m, produce):
        q = flip(f, m)
        produce(q)
        for j in range(upto):
            c, pos = rec[(j, m)]
            c.wait_recv()
            slabs[q] = (slabs[q].astype(F32) + rbufs[j][pos].astype(F32)).astype(BF16)

    wd_copy.wait()
    for c in pending:
        c.wait_send()
    pending.clear()

    def produce_y(q):
        def body(c, carry):
            at = pl.ds(pl.multiple_of(c * qw, qw), qw)
            v = dot(hid[...], wd[:, pl.ds(pl.multiple_of(q * quarter + c * qw, qw), qw)])
            ys[q, :, :, :, at] = v.astype(BF16).reshape(nd, half, 16, qw)
            return carry

        lax.fori_loop(0, n_qc, body, 0)

    def produce_x(q):
        def body(c, carry):
            at = pl.ds(pl.multiple_of(c * qw, qw), qw)
            v = dot_nt(dgr[...], wg[q, at, :]) + dot_nt(dur[...], wu[q, at, :])
            xs[q, :, :, :, at] = v.astype(BF16).reshape(nd, half, 16, qw)
            return carry

        lax.fori_loop(0, n_qc, body, 0)

    y_gen = reduce_scatter(ys, yr, produce_y)
    for _ in range(nf):
        next(y_gen)
    z = dot(hid[...], odm[0])

    def backward(c, carry):
        at = pl.ds(pl.multiple_of(c * cw, cw), cw)
        dh = SCALE * dot_nt(vq_s[...], odm[0, at, :])
        for q in range(nf):
            dh = dh + dot_nt(yb[q], wd[at, q * quarter : (q + 1) * quarter])
        g = gate[:, at]
        s = jax.nn.sigmoid(g)
        dgr[:, at] = (dh * up[:, at] * s * (1.0 + g * (1.0 - s))).astype(BF16)
        dur[:, at] = (dh * (g * s)).astype(BF16)
        return carry

    lax.fori_loop(0, n_hc, backward, 0)
    next(y_gen)
    w0 = dot_nt(dgr[...], iup[0, 0])
    w1 = dot_nt(dur[...], iup[0, 1])
    ar2 = all_reduce(
        compress(jnp.concatenate([z, w0, w1], axis=1)),
        [("f", b) for b in fbits] + [("d", b) for b in dbits], ar2s, ar2r,
    )
    next(ar2)
    x_gen = reduce_scatter(xs, xr, produce_x)
    zw = None
    for _ in range(nf):
        next(x_gen)
        if zw is None:
            zw = next(ar2)
    while zw is None:
        zw = next(ar2)
    next(x_gen)
    zw = expand(zw)
    qz_s[...] = zw[:, :ntr].astype(BF16)
    wq_s[...] = zw[:, ntr:].astype(BF16)

    mine = pl.ds(pl.multiple_of(d * rows_d, 16), rows_d)
    y_add = SCALE * dot(qz_s[mine, :], oum[0])
    x_add = SCALE * dot_nt(wq_s[mine, :], idm[0])
    y_own = next(y_gen) + y_add
    x_own = next(x_gen) + x_add
    for j in range(ne):
        at = slice(j * 8, j * 8 + 8)
        back[j] = jnp.concatenate([y_own[at], x_own[at]], axis=0).astype(BF16)
    home_own = pltpu.make_async_copy(back.at[e], home.at[e], lsem.at[2])
    home_own.start()
    got = []
    for j in range(1, ne):
        to = (e + j) % ne
        got.append(send(back.at[to], home.at[e], (d, to, f)))

    idg[0] = SCALE * dot_tn(xb[f], wq_s[...])
    oug[0] = SCALE * dot_tn(qz_s[...], yb[f])
    odg[0] = SCALE * dot_tn(hid[...], vq_s[...])
    iug[0, 0] = SCALE * dot_tn(q_s[:, :ntr], dgr[...])
    iug[0, 1] = SCALE * dot_tn(q_s[:, ntr:], dur[...])

    home_own.wait()
    for c in got:
        c.wait_recv()
    out = jnp.zeros((8, quarter), F32)
    grad = jnp.zeros((8, quarter), F32)
    for j in range(ne):
        v = home[j].astype(F32)
        out = out + wts[j, :, :1] * v[:8]
        grad = grad + v[8:]
    mixed[...] = out.astype(BF16)
    igrad[...] = grad.astype(BF16)
    for c in pending:
        c.wait_send()


def per_device(
    tokens, out_grad, expert_ids, tenant_ids, router_logits,
    gate_projection_weight, up_projection_weight, down_projection_weight,
    input_down_maps, input_up_maps, output_down_map, output_up_map,
):
    ne, nd, nf = lax.axis_size("expert"), lax.axis_size("dp"), lax.axis_size("ffn")
    tok, quarter = tokens.shape
    hidden = gate_projection_weight.shape[2]
    ntr = output_down_map.shape[2]
    rows_d = ne * tok
    rows = nd * rows_d
    first = jax.nn.sigmoid(router_logits[:, 0] - router_logits[:, 1])
    probs = jnp.stack([first, 1.0 - first], axis=1)
    hit = expert_ids[None] == jnp.arange(ne, dtype=jnp.int32)[:, None, None]
    member = jnp.any(hit, axis=2)
    weight = jnp.sum(jnp.where(hit, probs[None], 0.0), axis=2)
    x = jnp.where(member[:, :, None], tokens[None], jnp.zeros((), BF16))
    dy = (weight[:, :, None] * out_grad.astype(F32)[None]).astype(BF16)
    src = jnp.concatenate([x, dy], axis=1)
    column = jnp.arange(ntr, dtype=jnp.int32) // RANK
    msk = (member[:, :, None] & (tenant_ids[None, :, None] == column[None, None])).astype(F32)
    wts = jnp.broadcast_to(weight[:, :, None], (ne, tok, 128))

    fbits, dbits = bits_of(nf), bits_of(nd)
    rs_bufs = [pltpu.VMEM((nf >> (i + 1), nd, ne // 2, 16, quarter), BF16) for i in range(len(fbits))]
    rs_bufs += [pltpu.VMEM((nd >> (i + 1), ne // 2, 16, quarter), BF16) for i in range(len(dbits))]
    n_sem = (
        3 * (ne - 1) + 3 * nd + nf + 2 * (nf + nd) + 2 * len(fbits) + len(dbits)
    )
    n1, n2 = max(len(fbits), 1), max(len(fbits) + len(dbits), 1)
    vmem = pl.BlockSpec(memory_space=pltpu.VMEM)
    hbm = pl.BlockSpec(memory_space=pl.ANY)
    return pl.pallas_call(
        functools.partial(layer_kernel, nd, ne, nf),
        out_shape=(
            jax.ShapeDtypeStruct(tokens.shape, BF16),
            jax.ShapeDtypeStruct(tokens.shape, BF16),
            jax.ShapeDtypeStruct(input_down_maps.shape, F32),
            jax.ShapeDtypeStruct(input_up_maps.shape, F32),
            jax.ShapeDtypeStruct(output_down_map.shape, F32),
            jax.ShapeDtypeStruct(output_up_map.shape, F32),
        ),
        in_specs=[vmem] * 3 + [hbm] * 3 + [vmem] * 4,
        out_specs=[vmem] * 6,
        scratch_shapes=[
            pltpu.VMEM((nf, nd, ne, 2 * tok, quarter), BF16),
            pltpu.VMEM((nd, ne, tok, ntr), F32),
            pltpu.VMEM((nf, rows, quarter), BF16),
            pltpu.VMEM((nf, rows, quarter), BF16),
            pltpu.VMEM((nf, quarter, hidden), BF16),
            pltpu.VMEM((nf, quarter, hidden), BF16),
            pltpu.VMEM((hidden, nf * quarter), BF16),
            pltpu.VMEM((rows, hidden), F32),
            pltpu.VMEM((rows, hidden), F32),
            pltpu.VMEM((rows, hidden), BF16),
            pltpu.VMEM((rows, hidden), BF16),
            pltpu.VMEM((rows, hidden), BF16),
            pltpu.VMEM((rows, 2 * ntr), BF16),
            pltpu.VMEM((rows, ntr), BF16),
            pltpu.VMEM((rows, ntr), BF16),
            pltpu.VMEM((rows, 2 * ntr), BF16),
            pltpu.VMEM((ne, 2 * tok, quarter), BF16),
            pltpu.VMEM((ne, 2 * tok, quarter), BF16),
            pltpu.VMEM((n1, rows, 128), F32),
            pltpu.VMEM((n1, rows, 128), F32),
            pltpu.VMEM((n2, rows, 128), F32),
            pltpu.VMEM((n2, rows, 128), F32),
            *rs_bufs,
            *rs_bufs,
            pltpu.SemaphoreType.DMA((2 * nf + 1,)),
            pltpu.SemaphoreType.DMA((3,)),
            pltpu.SemaphoreType.DMA((n_sem,)),
            pltpu.SemaphoreType.DMA((n_sem,)),
        ],
        compiler_params=pltpu.CompilerParams(
            collective_id=0, has_side_effects=True, vmem_limit_bytes=67043328
        ),
    )(
        src, msk, wts,
        gate_projection_weight, up_projection_weight, down_projection_weight,
        input_down_maps, input_up_maps, output_down_map, output_up_map,
    )


def solution(mesh):
    return jax.shard_map(
        per_device,
        mesh=mesh,
        in_specs=(
            P(("dp", "expert"), "ffn"),
            P(("dp", "expert"), "ffn"),
            P(("dp", "expert"), None),
            P(("dp", "expert")),
            P(("dp", "expert"), None),
            P("expert", None, ("dp", "ffn")),
            P("expert", None, ("dp", "ffn")),
            P("expert", ("dp", "ffn"), None),
            P("expert", "ffn", None),
            P("expert", None, None, ("dp", "ffn")),
            P("expert", ("dp", "ffn"), None),
            P("expert", None, "ffn"),
        ),
        out_specs=(
            P(("dp", "expert"), "ffn"),
            P(("dp", "expert"), "ffn"),
            P("expert", "ffn", None),
            P("expert", None, None, ("dp", "ffn")),
            P("expert", ("dp", "ffn"), None),
            P("expert", None, "ffn"),
        ),
        check_vma=False,
    )
```

time: 313 us -> 91.2 us (0.29)
  local copies, waits for them, and re-layouts: 108 us -> 12.3 us
  matrix products: 72.1 us -> 0 us
  Pallas kernels: 0 us -> 71.8 us
  blocking collectives: 68 us -> 0 us
  starting transfers between devices: 25.4 us -> 0 us
  waiting for transfers between devices: 21 us -> 0 us
  between operations: 14.3 us -> 0.66 us
  other arithmetic: 2.48 us -> 5.9 us
    gather x12 -> x0, local copies, waits for them, and re-layouts: 86.1 us -> none  [the longest x3 27.9 us: per_device(): jnp.take(gate_cols, col_ids, axis=0)]
    dot_general x26 -> x0, matrix products: 72.1 us -> none  [the longest x8 17.5 us: matrix_product(): return jnp.dot(left, right, preferred_element_type=jnp.float32)]
    pallas_call x0 -> x1, Pallas kernels: none -> 71.8 us  [per_device(): pl.pallas_call(functools.partial(layer_kernel, nd, ne, nf), out_shape=(ja...]
    psum x2 -> x0, blocking collectives: 36.1 us -> none  [the longest x1 23.9 us: per_device(): lax.psum(matrix_product(hidden_state, output_down_map[0]), ('dp', 'ffn'))]
    all_gather x5 -> x0, blocking collectives: 32 us -> none  [the longest x1 8.58 us: per_device(): lax.all_gather(expert_grads, 'ffn', axis=2, tiled=True)]
    all_to_all x5 -> x0, starting transfers between devices: 25.1 us -> none  [the longest x1 6.35 us: per_device(): lax.all_to_all(tenant_send, 'expert', split_axis=0, concat_axis=0, tiled=...]
    reduce_scatter x2 -> x0, waiting for transfers between devices: 14.7 us -> none  [the longest x1 14.7 us: per_device(): lax.psum_scatter((gate_terms + up_terms).reshape(block_rows * lax.axis_si...]
    all_to_all x5 -> x0, waiting for transfers between devices: 6.33 us -> none  [the longest x1 5.03 us: per_device(): lax.all_to_all(input_result.reshape(n_experts, capacity, quarter), 'exper...]
  transfers between devices with their start and end apart: 7 -> 0, of which waited for: 3 -> 0; matrix products, arithmetic and copies ran while one was open for 44% -> 0% of each run, Pallas kernels for 0% -> 0%
where the time goes in v1:
time: 91.2 us; the launch traced here: 90.6 us
  Pallas kernels  71.8 us (79%)
  local copies, waits for them, and re-layouts  12.3 us (13%)
  other arithmetic  5.9 us (6%)
    pallas_call x1, Pallas kernels, per_device(): pl.pallas_call(functools.partial(layer_kernel, nd, ne, nf), out_shape=(ja...  71.8 us
    unnamed x6, local copies, waits for them, and re-layouts  11.6 us

profile of v1, /device:TPU:0, one launch (start us, length us, event | category | flops | bytes accessed | tf_op | source)
XLA Modules:
  0.0 90.6 jit_solution(8208741109204557587)
XLA Ops:
  0.6 0.7 fusion
  1.3 0.7 broadcast_compare_fusion
  2.1 0.8 broadcast_subtract_fusion
  2.8 0.7 select_reduce_fusion
  3.5 0.7 and_convert_fusion.msk
  4.2 0.7 broadcast_in_dim.53.wts
  4.9 0.7 convert_element_type.9
  5.6 0.1 multiply_convert_fusion
  5.7 0.8 broadcast_select_fusion
  6.5 0.7 pad_maximum_fusion.src
  7.2 71.8 %shard_map.163 = (bf16[8,1536]{1,0:T(8,128)(2,1)}, bf16[8,1536]{1,0:T(8,128)(2,1)}, f32[1,1536,256]{2,1,0:T(8,128)}, f32[1,2,128,1024]{3,2,1,0:T(8,128)}, f32[1,...) custom-call(bf16[4,16,1536]{2,1,0:T(8,128)(2,1)} %pad_maximum_fusion.src, f32[4,8,128]{2,1,0:T(8,128)} %and_convert_fusion.msk, ...), custom_call_target="tpu_custom_call" | custom-call | tf_op jit(solution)/shard_map/pallas_call | solution.py:424
  79.0 1.3 %copy.26 = bf16[8,1536]{1,0:T(8,128)(2,1)} copy(bf16[8,1536]{1,0:T(8,128)(2,1)} %get-tuple-element.14) | data formatting | bytes 49152
  80.4 1.3 %copy.27 = bf16[8,1536]{1,0:T(8,128)(2,1)} copy(bf16[8,1536]{1,0:T(8,128)(2,1)} %get-tuple-element.15) | data formatting | bytes 49152
  81.7 2.7 %copy.28 = f32[1,1536,256]{2,1,0:T(8,128)} copy(f32[1,1536,256]{2,1,0:T(8,128)} %get-tuple-element.16) | data formatting | bytes 3145728
  84.4 2.3 %copy.29 = f32[1,2,128,1024]{3,2,1,0:T(8,128)} copy(f32[1,2,128,1024]{3,2,1,0:T(8,128)} %get-tuple-element.17) | data formatting | bytes 2097152
  86.7 1.9 %copy.30 = f32[1,1024,128]{2,1,0:T(8,128)} copy(f32[1,1024,128]{2,1,0:T(8,128)} %get-tuple-element.18) | data formatting | bytes 1048576
  88.5 2.1 %copy.31 = f32[1,128,1536]{2,1,0:T(8,128)} copy(f32[1,128,1536]{2,1,0:T(8,128)} %get-tuple-element.19) | data formatting | bytes 1572864
  (2 shorter events, 0.0 us)
